TPU v7x, 32 devices: a whole 2x2x4 slice. The times are simulated.
32 devices in a mesh: img: 4 (over x, core), patch: 8 (over z, y).
Axes of the slice: x: 2, y: 2, z: 4, core: 2. Of those that a mesh axis runs over, the one named last changes fastest.
Arguments:
- hidden: bfloat16 [8, 8, 128, 640], P('img', 'patch'), may hold values from -100 to 100
- stale_attn_in: bfloat16 [8, 8, 128, 640], P('img', 'patch'), may hold values from -100 to 100
- stale_conv_in: bfloat16 [8, 8, 128, 640], P('img', 'patch'), may hold values from -6 to 6
- ln_gain: float32 [640], replicated, may hold values from 0.25 to 1.75
- ln_bias: float32 [640], replicated, may hold values from -2 to 2
- w_qkv: bfloat16 [640, 1920], replicated, may hold values from -3 to 3
- w_out: bfloat16 [640, 640], replicated, may hold values from -0.25 to 0.25
- gn_gain: float32 [640], replicated, may hold values from 0.25 to 1.75
- gn_bias: float32 [640], replicated, may hold values from -1.5 to 1.5
- conv_weight: bfloat16 [3, 3, 640, 640], replicated, may hold values from -0.078125 to 0.078125
- conv_bias: float32 [640], replicated, may hold values from -1.5 to 1.5
- time_shift: float32 [8, 640], P('img'), may hold values from -6 to 6
Outputs:
- block_out: bfloat16 [8, 8, 128, 640], P('img', 'patch')
All inputs are finite; a program needn't handle non-finite values.
Results may differ from a plain program's by a relative error of at most 0.0075.
The roundings to bfloat16 on the way count: a program that leaves them out, or rounds other values in their place, can miss the bound.
Values may be sent and summed in bfloat16 or wider, within the bound.
A program may use at most 128 MiB of HBM per device.

v0:
```python
import jax
import jax.numpy as jnp
from jax import lax
from jax.sharding import PartitionSpec as P

GROUPS = 32
HEAD_DIM = 64
EPSILON = 1e-05


def extended(block, sides, width):
    for axis, dim in sides:
        count = lax.axis_size(axis)
        forward = [(i, i + 1) for i in range(count - 1)]
        backward = [(target, source) for source, target in forward]
        low = lax.ppermute(
            lax.slice_in_dim(block, block.shape[dim] - width, None, axis=dim), axis, forward
        )
        high = lax.ppermute(lax.slice_in_dim(block, 0, width, axis=dim), axis, backward)
        block = jnp.concatenate([low, block, high], axis=dim)
    return block


def layer_norm(values, gain, bias):
    values = values.astype(jnp.float32)
    centre = jnp.mean(values, -1, keepdims=True)
    centred = values - centre
    spread = jnp.mean(centred * centred, -1, keepdims=True)
    return (centred * lax.rsqrt(spread + EPSILON) * gain + bias).astype(jnp.bfloat16)


def absorb(softmax_state, queries, key_rows, value_rows, blocked):
    running_max, weight_sum, accum = softmax_state
    samples, key_count, channels = key_rows.shape
    head_count = channels // HEAD_DIM
    keys_split = key_rows.reshape(samples, key_count, head_count, HEAD_DIM)
    values_split = value_rows.reshape(samples, key_count, head_count, HEAD_DIM)
    scores = jnp.einsum(
        "sqhd,skhd->shqk", queries, keys_split, preferred_element_type=jnp.float32
    ) * HEAD_DIM ** (-0.5)
    scores = jnp.where(blocked[None, None, None, :], -jnp.inf, scores)
    new_max = jnp.maximum(running_max, jnp.max(scores, -1))
    rescale = jnp.exp(running_max - new_max)
    weights = jnp.exp(scores - new_max[..., None])
    weight_sum = weight_sum * rescale + jnp.sum(weights, -1)
    accum = accum * rescale[..., None] + jnp.einsum(
        "shqk,skhd->shqd",
        weights.astype(jnp.bfloat16),
        values_split,
        preferred_element_type=jnp.float32,
    )
    return (new_max, weight_sum, accum)


def shards(
    hidden,
    stale_attn_in,
    stale_conv_in,
    ln_gain,
    ln_bias,
    w_qkv,
    w_out,
    gn_gain,
    gn_bias,
    conv_weight,
    conv_bias,
    time_shift,
):
    samples, rows_dev, col_count, channels = hidden.shape
    head_count = channels // HEAD_DIM
    local_count = rows_dev * col_count
    own_start = lax.axis_index("patch") * local_count
    fresh_in = layer_norm(hidden, ln_gain, ln_bias).reshape(samples, local_count, channels)
    stale_in = layer_norm(stale_attn_in, ln_gain, ln_bias).reshape(samples, local_count, channels)
    fresh_qkv = jnp.einsum(
        "stc,cd->std", fresh_in, w_qkv, preferred_element_type=jnp.float32
    ).astype(jnp.bfloat16)
    queries = fresh_qkv[..., :channels].reshape(samples, local_count, head_count, HEAD_DIM)
    w_pair = w_qkv[:, channels:]
    initial = (
        jnp.full((samples, head_count, local_count), -jnp.inf, jnp.float32),
        jnp.zeros((samples, head_count, local_count), jnp.float32),
        jnp.zeros((samples, head_count, local_count, HEAD_DIM), jnp.float32),
    )
    no_block = jnp.zeros((local_count,), bool)
    softmax_state = absorb(
        initial,
        queries,
        fresh_qkv[..., channels : 2 * channels],
        fresh_qkv[..., 2 * channels :],
        no_block,
    )
    block_rows = lax.all_gather(stale_in, "patch", axis=1, tiled=True)
    pair_rows = jnp.einsum(
        "snc,cd->snd", block_rows, w_pair, preferred_element_type=jnp.float32
    ).astype(jnp.bfloat16)
    positions = jnp.arange(block_rows.shape[1], dtype=jnp.int32)
    blocked = (positions >= own_start) & (positions < own_start + local_count)
    softmax_state = absorb(
        softmax_state, queries, pair_rows[..., :channels], pair_rows[..., channels:], blocked
    )
    running_max, weight_sum, accum = softmax_state
    attended = (
        (accum / weight_sum[..., None])
        .transpose(0, 2, 1, 3)
        .reshape(samples, local_count, channels)
        .astype(jnp.bfloat16)
    )
    attention_out = jnp.einsum("stc,cd->std", attended, w_out, preferred_element_type=jnp.float32)
    residual = (
        hidden.reshape(samples, local_count, channels).astype(jnp.float32) + attention_out
    ).astype(jnp.bfloat16)
    grouped = residual.astype(jnp.float32).reshape(samples, local_count, GROUPS, channels // GROUPS)
    cell_count = lax.axis_size("patch") * local_count * (channels // GROUPS)
    group_mean = lax.psum(jnp.sum(grouped, axis=(1, 3)), "patch") / cell_count
    centred = grouped - group_mean[:, None, :, None]
    group_var = lax.psum(jnp.sum(centred * centred, axis=(1, 3)), "patch") / cell_count
    normalized = (centred * lax.rsqrt(group_var + EPSILON)[:, None, :, None]).reshape(
        samples, local_count, channels
    )
    activated = (
        jax.nn.silu(normalized * gn_gain + gn_bias)
        .astype(jnp.bfloat16)
        .reshape(samples, rows_dev, col_count, channels)
    )
    stale_framed = extended(stale_conv_in, (("patch", 1),), 1)
    framed = jnp.concatenate([stale_framed[:, :1], activated, stale_framed[:, rows_dev + 1 :]], 1)
    framed = jnp.pad(framed, ((0, 0), (0, 0), (1, 1), (0, 0)))
    windows = [
        framed[:, tap_row : tap_row + rows_dev, tap_col : tap_col + col_count, :]
        for tap_row in range(3)
        for tap_col in range(3)
    ]
    unfolded = jnp.concatenate(windows, -1).reshape(samples * local_count, 9 * channels)
    convolved = jnp.dot(
        unfolded, conv_weight.reshape(9 * channels, channels), preferred_element_type=jnp.float32
    )
    summed_out = (
        convolved.reshape(samples, rows_dev, col_count, channels)
        + conv_bias
        + time_shift[:, None, None, :]
        + residual.astype(jnp.float32).reshape(samples, rows_dev, col_count, channels)
    )
    return summed_out.astype(jnp.bfloat16)


def solution(mesh):
    in_specs = (
        P("img", "patch", None, None),
        P("img", "patch", None, None),
        P("img", "patch", None, None),
        P(),
        P(),
        P(),
        P(),
        P(),
        P(),
        P(),
        P(),
        P("img", None),
    )
    out_specs = P("img", "patch", None, None)
    return jax.shard_map(shards, mesh=mesh, in_specs=in_specs, out_specs=out_specs, check_vma=False)
```

profile of v0, /device:TPU:0, one launch (start us, length us, event | category | flops | bytes accessed | tf_op | source)
XLA Modules:
  0.0 154.2 jit_solution(17788992651743523699)
XLA Ops:
  6.5 1.2 convert_reduce_fusion.1
  7.7 1.2 fusion.54
  8.9 1.9 %fusion.57 = bf16[2,1,128,640]{3,2,0,1:T(8,128)(2,1)} fusion(bf16[2,1,128,640]{3,2,1,0:T(8,128)(2,1)} %param.13, f32[2,128]{1,0:T(2,128)S(1)} %add_rsqrt_fusion.1, f32[2,128]{1,0:T(2,128)S(1)} %broadcast_multiply_fusion.1, f32[640]{0:T(1024)} %param.16, f32[640]{0:T(1024)} %param.15), kind=kLoop, calls=%fused_computation.59 | loop fusion | flops 983040 | bytes 662528 | tf_op jit(solution)/shard_map/convert_element_type | solution.py:29
  10.9 1.3 collective-permute-start.1
  12.2 6.3 %collective-permute-start = (bf16[2,1,128,640]{3,2,0,1:T(8,128)(2,1)}, bf16[2,1,128,640]{3,2,0,1:T(8,128)(2,1)}, u32[]{:S(2)}, u32[]{:S(2)}) collective-permute-start(bf16[2,1,128,640]{3,2,0,1:T(8,128)(2,1)} %bitcast.117), channel_id=1, source_target_pairs={{0,1},{1,2},{2,3},{3,4},{4,5},{5,6},{6,7},{8,9},{9,10},{10,11},{11... | collective-permute-start | bytes 983048 | tf_op jit(solution)/shard_map/ppermute | solution.py:16
  18.5 1.1 convert_reduce_fusion
  19.6 1.2 fusion.50
  20.8 3.0 %convolution_convert_fusion.1 = bf16[2,128,1920]{2,1,0:T(8,128)(2,1)S(1)} fusion(bf16[640,1920]{1,0:T(8,128)(2,1)} %param.17, bf16[2,1,128,640]{3,2,1,0:T(8,128)(2,1)} %param.12, f32[640]{0:T(1024)} %param.16, f32[640]{0:T(1024)} %param.15, f32[2,128]{1,0:T(2,128)S(1)} %add_rsqrt_fusion.2, f32[2,128]{1,0:T(2,128)S(1)} %broadcast_multiply_fusion.2), kind=kOutput, calls=%fused_computation.13 | convolution fusion | flops 630620160 | bytes 3775488 | tf_op jit(solution)/shard_map/stc,cd->std/dot_general | solution.py:75
  23.9 0.2 copy.28
  24.1 0.2 copy.29
  24.4 0.9 copy.30
  25.3 0.4 fusion.78
  25.7 1.1 copy-done.1
  27.0 46.8 %all-gather.3.cloned.1.call-done = bf16[2,1,1024,640]{3,2,0,1:T(8,128)(2,1)} async-done(((bf16[2,1,128,640]{3,2,0,1:T(8,128)(2,1)}), bf16[2,1,1024,640]{3,2,0,1:T(8,128)(2,1)}) %all-gather.3.cloned.1.call-update) | async-done | bytes 2621456 | tf_op jit(solution)/shard_map/all_gather | solution.py:93
  73.9 6.5 %convolution_convert_fusion = bf16[2,1024,1280]{2,1,0:T(8,128)(2,1)S(1)} fusion(bf16[2,1,1024,640]{3,2,0,1:T(8,128)(2,1)} %all-gather.3.cloned.1.call-done, bf16[640,1920]{1,0:T(8,128)(2,1)} %param.17), kind=kOutput, calls=%fused_computation.5 | convolution fusion | flops 3358064640 | bytes 9502720 | tf_op jit(solution)/shard_map/snc,cd->snd/dot_general | solution.py:94
  80.3 2.0 %fusion.76 = (bf16[2,1024,640]{2,1,0:T(8,128)(2,1)S(1)}, bf16[2,1024,640]{2,1,0:T(8,128)(2,1)}) fusion(bf16[2,1024,1280]{2,1,0:T(8,128)(2,1)S(1)} %convolution_convert_fusion), kind=kLoop, calls=%fused_computation.98 | loop fusion | bytes 10485760 | tf_op jit(solution)/shard_map/slice | solution.py:100
  82.3 4.5 %copy.34 = bf16[2,1024,640]{1,2,0:T(8,128)(2,1)} copy(bf16[2,1024,640]{2,1,0:T(8,128)(2,1)} %get-tuple-element.8) | data formatting | bytes 5242880 | tf_op jit(solution)/shard_map/slice | solution.py:100
  86.9 2.7 %copy.33 = bf16[2,1024,640]{1,2,0:T(8,128)(2,1)} copy(bf16[2,1024,640]{2,1,0:T(8,128)(2,1)S(1)} %get-tuple-element.7) | data formatting | bytes 5242880 | tf_op jit(solution)/shard_map/slice | solution.py:100
  89.6 3.5 %fusion = (f32[2,10,128]{2,1,0:T(8,128)S(1)}, f32[2,10,128,1024]{3,2,1,0:T(8,128)S(1)}) fusion(pred[1024]{0:T(1024)(128)(4,1)S(1)} %fusion.72, bf16[2,128,10,64]{1,3,2,0:T(8,128)(2,1)} %bitcast.110, bf16[2,1024,10,64]{1,3,2,0:T(8,128)(2,1)} %bitcast.108), kind=kOutput, calls=%fused_computation.2 | convolution fusion | flops 343406080 | bytes 13446144 | tf_op jit(solution)/shard_map/sqhd,skhd->shqk/dot_general | solution.py:38
  93.1 2.5 %fusion.1 = f32[2,10,128]{2,1,0:T(8,128)S(1)} fusion(f32[2,10,128,1024]{3,2,1,0:T(8,128)S(1)} %get-tuple-element.16, f32[2,10,128]{2,1,0:T(8,128)S(1)} %max.18, pred[1024]{0:T(1024)(128)(4,1)S(1)} %fusion.72), kind=kLoop, calls=%fused_computation.3 | loop fusion | flops 10483200 | bytes 10507264 | tf_op jit(solution)/shard_map/reduce_sum | solution.py:45
  95.6 2.4 %fusion.13 = f32[2,128,10,64]{1,3,2,0:T(8,128)S(1)} fusion(bf16[2,1024,10,64]{1,3,2,0:T(8,128)(2,1)S(1)} %bitcast.111, f32[2,10,128,1024]{3,2,1,0:T(8,128)S(1)} %get-tuple-element.16, f32[2,10,128]{2,1,0:T(8,128)S(1)} %max.18, pred[1024]{0:T(1024)(128)(4,1)S(1)} %fusion.72), kind=kOutput, calls=%fused_computation.20 | convolution fusion | flops 346030080 | bytes 13773824 | tf_op jit(solution)/shard_map/shqk,skhd->shqd/dot_general | solution.py:46
  98.1 0.4 fusion.31
  98.5 0.5 copy-done.4
  99.0 0.5 fusion.79
  99.7 19.0 %psum.14 = f32[2,32]{1,0:T(2,128)S(1)} all-reduce(f32[2,32]{1,0:T(2,128)S(1)} %reduce_sum.100), channel_id=1, replica_groups=mesh['img'=4,'patch'=8] {'patch'}, use_global_device_ids=true, to_apply=%region_10.11 | all-reduce | flops 64 | bytes 512 | tf_op jit(solution)/shard_map/psum | solution.py:115
  119.2 17.2 %psum.15 = f32[2,32]{1,0:T(2,128)S(1)} all-reduce(f32[2,32]{1,0:T(2,128)S(1)} %reduce_sum.103), channel_id=1, replica_groups=mesh['img'=4,'patch'=8] {'patch'}, use_global_device_ids=true, to_apply=%region_13.14 | all-reduce | flops 64 | bytes 512 | tf_op jit(solution)/shard_map/psum | solution.py:117
  136.6 0.2 fusion.67
  136.9 1.3 fusion.44
  138.3 1.0 constant_dynamic-update-slice_fusion.2
  139.5 0.3 constant_dynamic-update-slice_fusion.1
  139.9 1.0 constant_dynamic-update-slice_fusion
  141.0 6.4 %fusion.38 = bf16[2,1,128,640]{3,2,1,0:T(8,128)(2,1)} fusion(f32[2,128,640]{2,1,0:T(8,128)S(1)} %get-tuple-element.18, bf16[5760,640,1]{1,0,2:T(8,128)(2,1)} %bitcast.115, bf16[2,1,128,5760]{3,2,0,1:T(8,128)(2,1)S(1)} %slice_dynamic-update-slice_fusion, f32[2,640]{1,0:T(2,128)S(1)} %copy-done.9, f32[640]{0:T(1024)S(1)} %copy-done.10), kind=kOutput, calls=%fused_computation.37 | convolution fusion | flops 1888092160 | bytes 11312640 | tf_op jit(solution)/shard_map/dot_general | solution.py:135
  (50 shorter events, 1.7 us)
Async XLA Ops:
  6.5 91.9 %copy-start = (bf16[640,640]{1,0:T(8,128)(2,1)S(1)}, bf16[640,640]{1,0:T(8,128)(2,1)}, u32[]{:S(2)}) copy-start(bf16[640,640]{1,0:T(8,128)(2,1)} %param.18) | copy-start | bytes 2457604
  6.5 67.3 %all-gather.3.cloned.1.call-start = ((), (), s32[]{:S(2)}) async-start(), calls=%async_computation | async-start | bytes 2949120 | tf_op jit(solution)/shard_map/all_gather | solution.py:93
  10.9 126.0 %collective-permute-start.1 = (bf16[2,1,128,640]{3,2,0,1:T(8,128)(2,1)}, bf16[2,1,128,640]{3,2,0,1:T(8,128)(2,1)}, u32[]{:S(2)}, u32[]{:S(2)}) collective-permute-start(bf16[2,1,128,640]{3,2,0,1:T(8,128)(2,1)} %bitcast.116), channel_id=1, source_target_pairs={{1,0},{2,1},{3,2},{4,3},{5,4},{6,5},{7,6},{9,8},{10,9},{11,10},{12... | collective-permute-start | bytes 983048 | tf_op jit(solution)/shard_map/ppermute | solution.py:19
  12.2 124.7 %collective-permute-start = (bf16[2,1,128,640]{3,2,0,1:T(8,128)(2,1)}, bf16[2,1,128,640]{3,2,0,1:T(8,128)(2,1)}, u32[]{:S(2)}, u32[]{:S(2)}) collective-permute-start(bf16[2,1,128,640]{3,2,0,1:T(8,128)(2,1)} %bitcast.117), channel_id=1, source_target_pairs={{0,1},{1,2},{2,3},{3,4},{4,5},{5,6},{6,7},{8,9},{9,10},{10,11},{11... | collective-permute-start | bytes 983048 | tf_op jit(solution)/shard_map/ppermute | solution.py:16
  24.1 49.7 %copy-start.3 = (bf16[2,128,640]{1,2,0:T(8,128)(2,1)}, bf16[2,128,640]{1,2,0:T(8,128)(2,1)S(1)}, u32[]{:S(2)}) copy-start(bf16[2,128,640]{1,2,0:T(8,128)(2,1)S(1)} %copy.28) | copy-start | bytes 983044
  25.7 1.1 copy-start.1
  93.1 2.5 %copy-start.5 = (bf16[2,1024,640]{1,2,0:T(8,128)(2,1)S(1)}, bf16[2,1024,640]{1,2,0:T(8,128)(2,1)}, u32[]{:S(2)}) copy-start(bf16[2,1024,640]{1,2,0:T(8,128)(2,1)} %copy.34) | copy-start | bytes 7864324
  95.6 2.4 %copy-start.2 = (f32[2,10,128,128]{2,3,1,0:T(8,128)S(1)}, f32[2,10,128,128]{2,3,1,0:T(8,128)}, u32[]{:S(2)}) copy-start(f32[2,10,128,128]{2,3,1,0:T(8,128)} %copy-done.1) | copy-start | bytes 3932164
  95.6 2.4 %copy-start.6 = (bf16[2,128,640]{1,2,0:T(8,128)(2,1)S(1)}, bf16[2,128,640]{1,2,0:T(8,128)(2,1)}, u32[]{:S(2)}) copy-start(bf16[2,128,640]{1,2,0:T(8,128)(2,1)} %copy.30) | copy-start | bytes 983044
  98.0 1.0 copy-start.4
  98.1 38.6 %copy-start.7 = (f32[640]{0:T(1024)S(1)}, f32[640]{0:T(1024)}, u32[]{:S(2)}) copy-start(f32[640]{0:T(1024)} %param.20) | copy-start | bytes 7684
  98.1 38.6 %copy-start.8 = (f32[640]{0:T(1024)S(1)}, f32[640]{0:T(1024)}, u32[]{:S(2)}) copy-start(f32[640]{0:T(1024)} %param.19) | copy-start | bytes 7684
  138.3 2.7 %copy-start.9 = (f32[2,640]{1,0:T(2,128)S(1)}, f32[2,640]{1,0:T(2,128)}, u32[]{:S(2)}) copy-start(f32[2,640]{1,0:T(2,128)} %param.23) | copy-start | bytes 15364
  138.3 2.7 %copy-start.10 = (f32[640]{0:T(1024)S(1)}, f32[640]{0:T(1024)}, u32[]{:S(2)}) copy-start(f32[640]{0:T(1024)} %param.22) | copy-start | bytes 7684
Sparse Core Ops, SparseCore 0:
  11.0 62.8 all-gather.2
where the time goes:
time: 155 us; the launch traced here: 154 us
  waiting for transfers between devices  46.9 us (30%)
  blocking collectives  36.2 us (23%)
  matrix products  23 us (15%)
  local copies, waits for them, and re-layouts  15.4 us (10%)
  between operations  13.7 us (9%)
  other arithmetic  11.4 us (7%)
  starting transfers between devices  7.56 us (5%)
    all_gather x1, waiting for transfers between devices, shards(): block_rows = lax.all_gather(stale_in, 'patch', axis=1, tiled=True)  46.8 us
    psum x1, blocking collectives, shards(): group_mean = lax.psum(jnp.sum(grouped, axis=(1, 3)), 'patch') / cell_count  19 us
    psum x1, blocking collectives, shards(): lax.psum(jnp.sum(centred * centred, axis=(1, 3)), 'patch') / cell_count  17.2 us
    dot_general x1, matrix products, shards(): jnp.einsum('snc,cd->snd', block_rows, w_pair, preferred_element_type=jnp....  6.47 us
    dot_general x1, matrix products, shards(): jnp.dot(unfolded, conv_weight.reshape(9 * channels, channels), preferred_...  6.35 us
    ppermute x1, starting transfers between devices, extended(): lax.ppermute(lax.slice_in_dim(block, block.shape[dim] - width, None, axis...  6.26 us
    slice x2, local copies, waits for them, and re-layouts, shards(): pair_rows[..., :channels]  4.69 us
    slice x1, local copies, waits for them, and re-layouts, shards(): pair_rows[..., channels:]  4.54 us
  transfers between devices with their start and end apart: 3, of which 1 were waited for; matrix products, arithmetic and copies ran while one was open for 22% of the time, Pallas kernels for 0%

commit v1 on v0

--- a/solution.py
+++ b/solution.py
@@ -90,7 +90,7 @@
         fresh_qkv[..., 2 * channels :],
         no_block,
     )
-    block_rows = lax.all_gather(stale_in, "patch", axis=1, tiled=True)
+    block_rows = jnp.concatenate(lax.all_gather(stale_in, "patch"), axis=1)
     pair_rows = jnp.einsum(
         "snc,cd->snd", block_rows, w_pair, preferred_element_type=jnp.float32
     ).astype(jnp.bfloat16)

time: 155 us -> 155 us (level)
  local copies, waits for them, and re-layouts: 15.4 us -> 17.9 us
  matrix products: 23 us -> 21 us
    all_gather x0 -> x1, local copies, waits for them, and re-layouts: none -> 2.16 us  [shards(): block_rows = jnp.concatenate(lax.all_gather(stale_in, 'patch'), axis=1)]
    dot_general x1, matrix products: 6.47 us -> 4.47 us  [shards(): jnp.einsum('snc,cd->snd', block_rows, w_pair, preferred_element_type=jnp....]
    unnamed x29 -> x31, local copies, waits for them, and re-layouts: 4.02 us -> 4.33 us
where the time goes in v1:
time: 155 us
  waiting for transfers between devices  46.9 us (30%)
  blocking collectives  36.4 us (23%)
  matrix products  21 us (14%)
  local copies, waits for them, and re-layouts  17.9 us (12%)
  between operations  13.7 us (9%)
  other arithmetic  11.4 us (7%)
  starting transfers between devices  7.56 us (5%)
    all_gather x1, waiting for transfers between devices, shards(): block_rows = jnp.concatenate(lax.all_gather(stale_in, 'patch'), axis=1)  46.9 us
    psum x1, blocking collectives, shards(): group_mean = lax.psum(jnp.sum(grouped, axis=(1, 3)), 'patch') / cell_count  19 us
    psum x1, blocking collectives, shards(): lax.psum(jnp.sum(centred * centred, axis=(1, 3)), 'patch') / cell_count  17.4 us
    dot_general x1, matrix products, shards(): jnp.dot(unfolded, conv_weight.reshape(9 * channels, channels), preferred_...  6.36 us
    ppermute x1, starting transfers between devices, extended(): lax.ppermute(lax.slice_in_dim(block, block.shape[dim] - width, None, axis...  6.26 us
    slice x2, local copies, waits for them, and re-layouts, shards(): pair_rows[..., :channels]  4.69 us
    slice x1, local copies, waits for them, and re-layouts, shards(): pair_rows[..., channels:]  4.54 us
    dot_general x1, matrix products, shards(): jnp.einsum('snc,cd->snd', block_rows, w_pair, preferred_element_type=jnp....  4.47 us
  transfers between devices with their start and end apart: 3, of which 1 were waited for; matrix products, arithmetic and copies ran while one was open for 22% of the time, Pallas kernels for 0%

profile of v1, /device:TPU:0, one launch (start us, length us, event | category | flops | bytes accessed | tf_op | source)
XLA Modules:
  0.0 154.9 jit_solution(299765751489458605)
XLA Ops:
  6.5 1.2 convert_reduce_fusion.1
  7.7 1.2 fusion.53
  8.9 1.9 %fusion.59 = bf16[2,1,128,640]{3,2,1,0:T(8,128)(2,1)} fusion(bf16[2,1,128,640]{3,2,1,0:T(8,128)(2,1)} %param.13, f32[2,128]{1,0:T(2,128)S(1)} %add_rsqrt_fusion.1, f32[2,128]{1,0:T(2,128)S(1)} %broadcast_multiply_fusion.1, f32[640]{0:T(1024)} %param.16, f32[640]{0:T(1024)} %param.15), kind=kLoop, calls=%fused_computation.62 | loop fusion | flops 983040 | bytes 662528 | tf_op jit(solution)/shard_map/convert_element_type | solution.py:29
  10.9 1.3 collective-permute-start.1
  12.2 6.3 %collective-permute-start = (bf16[2,1,128,640]{3,2,0,1:T(8,128)(2,1)}, bf16[2,1,128,640]{3,2,0,1:T(8,128)(2,1)}, u32[]{:S(2)}, u32[]{:S(2)}) collective-permute-start(bf16[2,1,128,640]{3,2,0,1:T(8,128)(2,1)} %bitcast.123), channel_id=1, source_target_pairs={{0,1},{1,2},{2,3},{3,4},{4,5},{5,6},{6,7},{8,9},{9,10},{10,11},{11... | collective-permute-start | bytes 983048 | tf_op jit(solution)/shard_map/ppermute | solution.py:16
  18.5 1.1 convert_reduce_fusion
  19.6 1.2 fusion.49
  20.8 3.0 %convolution_convert_fusion.1 = bf16[2,128,1920]{2,1,0:T(8,128)(2,1)S(1)} fusion(bf16[640,1920]{1,0:T(8,128)(2,1)} %param.17, bf16[2,1,128,640]{3,2,1,0:T(8,128)(2,1)} %param.12, f32[640]{0:T(1024)} %param.16, f32[640]{0:T(1024)} %param.15, f32[2,128]{1,0:T(2,128)S(1)} %add_rsqrt_fusion.2, f32[2,128]{1,0:T(2,128)S(1)} %broadcast_multiply_fusion.2), kind=kOutput, calls=%fused_computation.12 | convolution fusion | flops 630620160 | bytes 3775488 | tf_op jit(solution)/shard_map/stc,cd->std/dot_general | solution.py:75
  24.3 0.9 copy.44
  25.3 0.4 fusion.78
  25.7 1.1 copy-done.1
  27.0 46.9 %all-gather.3.cloned.1.call-done = bf16[16,1,128,640]{3,2,1,0:T(8,128)(2,1)} async-done(((bf16[2,1,128,640]{3,2,1,0:T(8,128)(2,1)}), bf16[16,1,128,640]{3,2,1,0:T(8,128)(2,1)}) %all-gather.3.cloned.1.call-update) | async-done | bytes 2621456 | tf_op jit(solution)/shard_map/all_gather | solution.py:93
  73.9 2.2 %copy.48 = bf16[8,2,128,640]{3,2,0,1:T(8,128)(2,1)S(1)} copy(bf16[8,2,128,640]{3,2,1,0:T(8,128)(2,1)} %bitcast.115) | data formatting | bytes 5242880 | tf_op jit(solution)/shard_map/all_gather | solution.py:93
  76.0 0.3 copy-done.9
  76.3 4.5 %convolution_convert_fusion = bf16[2,1024,1280]{2,1,0:T(8,128)(2,1)S(1)} fusion(bf16[2,1024,640]{2,1,0:T(8,128)(2,1)S(1)} %bitcast.117, bf16[640,1920]{1,0:T(8,128)(2,1)S(1)} %copy-done.9), kind=kOutput, calls=%fused_computation.5 | convolution fusion | flops 3358064640 | bytes 9502720 | tf_op jit(solution)/shard_map/snc,cd->snd/dot_general | solution.py:94
  80.8 2.0 %fusion.76 = (bf16[2,1024,640]{2,1,0:T(8,128)(2,1)S(1)}, bf16[2,1024,640]{2,1,0:T(8,128)(2,1)}) fusion(bf16[2,1024,1280]{2,1,0:T(8,128)(2,1)S(1)} %convolution_convert_fusion), kind=kLoop, calls=%fused_computation.98 | loop fusion | bytes 10485760 | tf_op jit(solution)/shard_map/slice | solution.py:100
  82.8 4.5 %copy.50 = bf16[2,1024,640]{1,2,0:T(8,128)(2,1)} copy(bf16[2,1024,640]{2,1,0:T(8,128)(2,1)} %get-tuple-element.8) | data formatting | bytes 5242880 | tf_op jit(solution)/shard_map/slice | solution.py:100
  87.3 2.7 %copy.49 = bf16[2,1024,640]{1,2,0:T(8,128)(2,1)} copy(bf16[2,1024,640]{2,1,0:T(8,128)(2,1)S(1)} %get-tuple-element.7) | data formatting | bytes 5242880 | tf_op jit(solution)/shard_map/slice | solution.py:100
  90.1 3.5 %fusion = (f32[2,10,128]{2,1,0:T(8,128)S(1)}, f32[2,10,128,1024]{3,2,1,0:T(8,128)S(1)}) fusion(pred[1024]{0:T(1024)(128)(4,1)S(1)} %fusion.72, bf16[2,128,10,64]{1,3,2,0:T(8,128)(2,1)} %bitcast.114, bf16[2,1024,10,64]{1,3,2,0:T(8,128)(2,1)} %bitcast.112), kind=kOutput, calls=%fused_computation.2 | convolution fusion | flops 343406080 | bytes 13446144 | tf_op jit(solution)/shard_map/sqhd,skhd->shqk/dot_general | solution.py:38
  93.6 2.5 %fusion.1 = f32[2,10,128]{2,1,0:T(8,128)S(1)} fusion(f32[2,10,128,1024]{3,2,1,0:T(8,128)S(1)} %get-tuple-element.16, f32[2,10,128]{2,1,0:T(8,128)S(1)} %max.18, pred[1024]{0:T(1024)(128)(4,1)S(1)} %fusion.72), kind=kLoop, calls=%fused_computation.3 | loop fusion | flops 10483200 | bytes 10507264 | tf_op jit(solution)/shard_map/reduce_sum | solution.py:45
  96.1 2.4 %fusion.12 = f32[2,128,10,64]{1,3,2,0:T(8,128)S(1)} fusion(bf16[2,1024,10,64]{1,3,2,0:T(8,128)(2,1)S(1)} %bitcast.116, f32[2,10,128,1024]{3,2,1,0:T(8,128)S(1)} %get-tuple-element.16, f32[2,10,128]{2,1,0:T(8,128)S(1)} %max.18, pred[1024]{0:T(1024)(128)(4,1)S(1)} %fusion.72), kind=kOutput, calls=%fused_computation.19 | convolution fusion | flops 346030080 | bytes 13773824 | tf_op jit(solution)/shard_map/shqk,skhd->shqd/dot_general | solution.py:46
  98.6 0.3 fusion.30
  98.9 0.5 copy-done.4
  99.4 0.5 fusion.79
  100.2 19.0 %psum.14 = f32[2,32]{1,0:T(2,128)S(1)} all-reduce(f32[2,32]{1,0:T(2,128)S(1)} %reduce_sum.100), channel_id=1, replica_groups=mesh['img'=4,'patch'=8] {'patch'}, use_global_device_ids=true, to_apply=%region_10.11 | all-reduce | flops 64 | bytes 512 | tf_op jit(solution)/shard_map/psum | solution.py:115
  119.6 17.4 %psum.15 = f32[2,32]{1,0:T(2,128)S(1)} all-reduce(f32[2,32]{1,0:T(2,128)S(1)} %reduce_sum.103), channel_id=1, replica_groups=mesh['img'=4,'patch'=8] {'patch'}, use_global_device_ids=true, to_apply=%region_13.14 | all-reduce | flops 64 | bytes 512 | tf_op jit(solution)/shard_map/psum | solution.py:117
  137.3 0.2 fusion.67
  137.5 1.3 fusion.43
  139.0 1.0 constant_dynamic-update-slice_fusion.2
  140.1 0.3 constant_dynamic-update-slice_fusion.1
  140.6 1.0 constant_dynamic-update-slice_fusion
  141.7 6.4 %fusion.37 = bf16[2,1,128,640]{3,2,1,0:T(8,128)(2,1)} fusion(f32[2,128,640]{2,1,0:T(8,128)S(1)} %get-tuple-element.18, bf16[5760,640,1]{1,0,2:T(8,128)(2,1)} %bitcast.121, bf16[2,1,128,5760]{3,2,0,1:T(8,128)(2,1)S(1)} %slice_dynamic-update-slice_fusion, f32[2,640]{1,0:T(2,128)S(1)} %copy-done.10, f32[640]{0:T(1024)S(1)} %copy-done.11), kind=kOutput, calls=%fused_computation.36 | convolution fusion | flops 1888092160 | bytes 11312640 | tf_op jit(solution)/shard_map/dot_general | solution.py:135
  (53 shorter events, 2.2 us)
Async XLA Ops:
  6.5 92.4 %copy-start = (bf16[640,640]{1,0:T(8,128)(2,1)S(1)}, bf16[640,640]{1,0:T(8,128)(2,1)}, u32[]{:S(2)}) copy-start(bf16[640,640]{1,0:T(8,128)(2,1)} %param.18) | copy-start | bytes 2457604
  6.5 67.3 %all-gather.3.cloned.1.call-start = ((), (), s32[]{:S(2)}) async-start(), calls=%async_computation | async-start | bytes 2949120 | tf_op jit(solution)/shard_map/all_gather | solution.py:93
  10.9 126.6 %collective-permute-start.1 = (bf16[2,1,128,640]{3,2,0,1:T(8,128)(2,1)}, bf16[2,1,128,640]{3,2,0,1:T(8,128)(2,1)}, u32[]{:S(2)}, u32[]{:S(2)}) collective-permute-start(bf16[2,1,128,640]{3,2,0,1:T(8,128)(2,1)} %bitcast.122), channel_id=1, source_target_pairs={{1,0},{2,1},{3,2},{4,3},{5,4},{6,5},{7,6},{9,8},{10,9},{11,10},{12... | collective-permute-start | bytes 983048 | tf_op jit(solution)/shard_map/ppermute | solution.py:19
  12.2 125.3 %collective-permute-start = (bf16[2,1,128,640]{3,2,0,1:T(8,128)(2,1)}, bf16[2,1,128,640]{3,2,0,1:T(8,128)(2,1)}, u32[]{:S(2)}, u32[]{:S(2)}) collective-permute-start(bf16[2,1,128,640]{3,2,0,1:T(8,128)(2,1)} %bitcast.123), channel_id=1, source_target_pairs={{0,1},{1,2},{2,3},{3,4},{4,5},{5,6},{6,7},{8,9},{9,10},{10,11},{11... | collective-permute-start | bytes 983048 | tf_op jit(solution)/shard_map/ppermute | solution.py:16
  24.1 51.9 %copy-start.3 = (bf16[2,128,640]{1,2,0:T(8,128)(2,1)}, bf16[2,128,640]{1,2,0:T(8,128)(2,1)S(1)}, u32[]{:S(2)}) copy-start(bf16[2,128,640]{1,2,0:T(8,128)(2,1)S(1)} %copy.42) | copy-start | bytes 983044
  25.7 1.1 copy-start.1
  73.9 2.5 %copy-start.9 = (bf16[640,1920]{1,0:T(8,128)(2,1)S(1)}, bf16[640,1920]{1,0:T(8,128)(2,1)}, u32[]{:S(2)}) copy-start(bf16[640,1920]{1,0:T(8,128)(2,1)} %param.17) | copy-start | bytes 7372804
  93.6 2.5 %copy-start.5 = (bf16[2,1024,640]{1,2,0:T(8,128)(2,1)S(1)}, bf16[2,1024,640]{1,2,0:T(8,128)(2,1)}, u32[]{:S(2)}) copy-start(bf16[2,1024,640]{1,2,0:T(8,128)(2,1)} %copy.50) | copy-start | bytes 7864324
  96.1 2.4 %copy-start.2 = (f32[2,10,128,128]{2,3,1,0:T(8,128)S(1)}, f32[2,10,128,128]{2,3,1,0:T(8,128)}, u32[]{:S(2)}) copy-start(f32[2,10,128,128]{2,3,1,0:T(8,128)} %copy-done.1) | copy-start | bytes 3932164
  96.1 2.4 %copy-start.6 = (bf16[2,128,640]{1,2,0:T(8,128)(2,1)S(1)}, bf16[2,128,640]{1,2,0:T(8,128)(2,1)}, u32[]{:S(2)}) copy-start(bf16[2,128,640]{1,2,0:T(8,128)(2,1)} %copy.44) | copy-start | bytes 983044
  98.5 1.0 copy-start.4
  98.5 38.8 %copy-start.7 = (f32[640]{0:T(1024)S(1)}, f32[640]{0:T(1024)}, u32[]{:S(2)}) copy-start(f32[640]{0:T(1024)} %param.20) | copy-start | bytes 7684
  98.5 38.7 %copy-start.8 = (f32[640]{0:T(1024)S(1)}, f32[640]{0:T(1024)}, u32[]{:S(2)}) copy-start(f32[640]{0:T(1024)} %param.19) | copy-start | bytes 7684
  138.9 2.7 %copy-start.10 = (f32[2,640]{1,0:T(2,128)S(1)}, f32[2,640]{1,0:T(2,128)}, u32[]{:S(2)}) copy-start(f32[2,640]{1,0:T(2,128)} %param.23) | copy-start | bytes 15364
  138.9 2.7 %copy-start.11 = (f32[640]{0:T(1024)S(1)}, f32[640]{0:T(1024)}, u32[]{:S(2)}) copy-start(f32[640]{0:T(1024)} %param.22) | copy-start | bytes 7684
Sparse Core Ops, SparseCore 0:
  11.0 62.8 all-gather.2
